TPU v7x, 32 devices: a whole 2x2x4 slice. The times are simulated.
32 devices in a mesh: mode: 4 (over y, x), mesh: 8 (over z, core).
Axes of the slice: x: 2, y: 2, z: 4, core: 2. Of those that a mesh axis runs over, the one named last changes fastest.
Arguments:
- velocity: float32 [3, 2, 64, 20480], P(None, None, 'mode', 'mesh'), may hold values from -2.1 to 2.1
- magnetic: float32 [3, 2, 64, 20480], P(None, None, 'mode', 'mesh'), may hold values from -2.1 to 2.1
- leaf_inverse: bfloat16 [64, 160, 128, 128], P('mode', 'mesh'), may hold values from -1 to 2
- leaf_coupling: bfloat16 [64, 128, 20480], P('mode', None, 'mesh'), may hold values from -0.05908203 to 0.05908203
- separator_inverse: bfloat16 [64, 1024, 128], P('mode', 'mesh'), may hold values from -1 to 2
- separator_coupling: bfloat16 [64, 1024, 128], P('mode', 'mesh'), may hold values from -0.26367188 to 0.26367188
- separator_source: float32 [2, 64, 1024], P(None, 'mode', 'mesh'), may hold values from -6 to 6
- front_rows: int32 [8, 2, 128], P('mesh'), may hold values from 0 to 127, each once within a row
Outputs:
- nonlinear: float32 [3, 2, 64, 20480], P(None, None, 'mode', 'mesh')
- azimuthal_field: float32 [2, 64, 20480], P(None, 'mode', 'mesh')
- separator_solution: float32 [2, 64, 1024], P(None, 'mode', 'mesh')
Inputs may be any that keep to these rules, and one draw needn't show every extreme that they name: front_rows[p, 0] and front_rows[p, 1] each hold every number below 128 once.
All inputs are finite; a program needn't handle non-finite values.
Results may differ from a plain program's by a relative error of at most 0.015.
Values may be sent and summed in bfloat16 or wider, within the bound.
No kernel may reach another device: no remote copies, remote signals or barrier semaphores. Data moves between devices by JAX's collectives and lax.ppermute only.
A program may use at most 128 MiB of HBM per device.

v0:
```python
import jax
import jax.numpy as jnp
from jax import lax
from jax.sharding import PartitionSpec as P

M = 64
NPHI = 192
highest = lax.Precision.HIGHEST
dt_step = 0.5


def tables():
    angles = jnp.arange(NPHI, dtype=jnp.int32)[:, None]
    orders = jnp.arange(M, dtype=jnp.int32)[None, :]
    phase = (angles * orders % NPHI).astype(jnp.float32) * (2.0 * jnp.pi / NPHI)
    forward = jnp.stack([jnp.cos(phase), jnp.sin(phase)], axis=1)
    weights = jnp.where(orders == 0, 1.0, 2.0).astype(jnp.float32) / NPHI
    backward = jnp.stack([(jnp.cos(phase) * weights).T, (jnp.sin(phase) * weights).T], axis=0)
    return (forward, backward)


def cross_terms(first, second):
    return jnp.stack(
        [
            first[1] * second[2] - first[2] * second[1],
            first[2] * second[0] - first[0] * second[2],
            first[0] * second[1] - first[1] * second[0],
        ]
    )


def forward_fields(forward, velocity, magnetic):
    return (
        jnp.einsum("kam,camn->ckn", forward, velocity, precision=highest),
        jnp.einsum("kam,camn->ckn", forward, magnetic, precision=highest),
    )


def gather_children(values):
    return lax.all_gather(values, "mesh", axis=2, tiled=True)


def gather_parents(values):
    return lax.all_gather(values, "mesh", axis=2, tiled=True)


def block_of(whole, index, partitions, sep_rows):
    start = (jnp.clip(index, 0, partitions - 1) * sep_rows).astype(jnp.int32)
    return lax.dynamic_slice_in_dim(whole, start, sep_rows, 2)


def shards(
    velocity,
    magnetic,
    leaf_inverse,
    leaf_coupling,
    separator_inverse,
    separator_coupling,
    separator_source,
    front_rows,
):
    modes_dev = velocity.shape[2]
    nodes_dev = velocity.shape[3]
    forward, backward = tables()
    spread_velocity, spread_magnetic = (
        lax.all_to_all(
            velocity.astype(jnp.bfloat16), "mode", split_axis=3, concat_axis=2, tiled=True
        ).astype(velocity.dtype),
        lax.all_to_all(
            magnetic.astype(jnp.bfloat16), "mode", split_axis=3, concat_axis=2, tiled=True
        ).astype(magnetic.dtype),
    )
    phys_velocity, phys_magnetic = forward_fields(forward, spread_velocity, spread_magnetic)
    local_terms = jnp.einsum(
        "amk,ckn->camn", backward, cross_terms(phys_velocity, phys_magnetic), precision=highest
    )
    nonlinear = lax.all_to_all(
        local_terms.astype(jnp.bfloat16), "mode", split_axis=2, concat_axis=3, tiled=True
    ).astype(local_terms.dtype)
    blocks_dev = leaf_inverse.shape[1]
    block_width = leaf_inverse.shape[2]
    sep_rows = separator_source.shape[2]
    source = (magnetic[1] + dt_step * nonlinear[1]).astype(jnp.bfloat16)
    leaf_solved = (
        jnp.einsum(
            "mkij,cmkj->cmki",
            leaf_inverse,
            source.reshape(2, modes_dev, blocks_dev, block_width),
            preferred_element_type=jnp.float32,
        )
        .reshape(2, modes_dev, nodes_dev)
        .astype(jnp.bfloat16)
    )
    row_order = front_rows[0]
    leaf_map = jnp.take(leaf_coupling, row_order[0], axis=1)
    upward_map = jnp.take(separator_coupling, row_order[1], axis=1)
    leaf_update = jnp.einsum(
        "mij,cmj->cmi", leaf_map, leaf_solved, preferred_element_type=jnp.float32
    )
    partitions = lax.axis_size("mesh")
    levels = partitions.bit_length() - 1
    position = lax.axis_index("mesh")
    depth_now = sum(
        [(position % 2**bit_now == 0).astype(jnp.int32) for bit_now in range(1, levels + 1)]
    )
    level_here = depth_now + 1

    def settle(arrived, height, reduced, outgoing):
        fresh = jnp.einsum(
            "mij,cmj->cmi",
            separator_inverse,
            (separator_source - arrived).astype(jnp.bfloat16),
            preferred_element_type=jnp.float32,
        ).astype(jnp.bfloat16)
        sending = jnp.einsum("mij,cmj->cmi", upward_map, fresh, preferred_element_type=jnp.float32)
        active = level_here == height
        return (jnp.where(active, fresh, reduced), jnp.where(active, sending, outgoing))

    reduced = jnp.zeros(separator_source.shape, jnp.bfloat16)
    outgoing = jnp.zeros(separator_source.shape, jnp.float32)
    everyone = gather_children(leaf_update)
    arrived = block_of(everyone, position - 1, partitions, sep_rows) + block_of(
        everyone, position, partitions, sep_rows
    )
    reduced, outgoing = settle(arrived, 1, reduced, outgoing)
    for height in range(2, levels + 1):
        gap = 2 ** (height - 2)
        everyone = gather_children(outgoing)
        arrived = block_of(everyone, position - gap, partitions, sep_rows) + block_of(
            everyone, position + gap, partitions, sep_rows
        )
        reduced, outgoing = settle(arrived, height, reduced, outgoing)
    everyone = gather_children(outgoing)
    reduced, outgoing = settle(
        block_of(everyone, partitions // 2, partitions, sep_rows), levels + 1, reduced, outgoing
    )
    top_value = jnp.einsum(
        "mij,cmi->cmj", separator_inverse, reduced, preferred_element_type=jnp.float32
    )
    solution = jnp.where(
        level_here == levels + 1, top_value, jnp.zeros(separator_source.shape, jnp.float32)
    )
    for height in range(levels, 0, -1):
        everyone = gather_parents(solution.astype(jnp.bfloat16))
        if height == levels:
            parent = position * 0
        else:
            parent = position // 2 ** (height + 1) * 2 ** (height + 1) + 2**height
        above = block_of(everyone, parent, partitions, sep_rows)
        residue = reduced.astype(jnp.float32) - jnp.einsum(
            "mij,cmi->cmj", upward_map, above, preferred_element_type=jnp.float32
        )
        fresh = jnp.einsum(
            "mij,cmi->cmj",
            separator_inverse,
            residue.astype(jnp.bfloat16),
            preferred_element_type=jnp.float32,
        )
        solution = jnp.where(level_here == height, fresh, solution)
    everyone = gather_parents(solution.astype(jnp.bfloat16))
    above = block_of(everyone, 2 * (position // 2) + 1, partitions, sep_rows)
    residue = leaf_solved.astype(jnp.float32) - jnp.einsum(
        "mij,cmi->cmj", leaf_map, above, preferred_element_type=jnp.float32
    )
    azimuthal_field = jnp.einsum(
        "mkji,cmkj->cmki",
        leaf_inverse,
        residue.astype(jnp.bfloat16).reshape(2, modes_dev, blocks_dev, block_width),
        preferred_element_type=jnp.float32,
    ).reshape(2, modes_dev, nodes_dev)
    return (nonlinear, azimuthal_field, solution)


def solution(mesh):
    in_specs = (
        P(None, None, "mode", "mesh"),
        P(None, None, "mode", "mesh"),
        P("mode", "mesh", None, None),
        P("mode", None, "mesh"),
        P("mode", "mesh", None),
        P("mode", "mesh", None),
        P(None, "mode", "mesh"),
        P("mesh", None, None),
    )
    out_specs = (P(None, None, "mode", "mesh"), P(None, "mode", "mesh"), P(None, "mode", "mesh"))
    return jax.shard_map(shards, mesh=mesh, in_specs=in_specs, out_specs=out_specs, check_vma=False)
```

profile of v0, /device:TPU:0, one launch (start us, length us, event | category | flops | bytes accessed | tf_op | source)
XLA Modules:
  0.0 205.2 jit_solution(15129035748217924793)
XLA Ops:
  2.0 5.2 %copy.84 = bf16[3,2,16,2560]{2,0,1,3:T(4,128)(2,1)} copy(bf16[3,2,16,2560]{3,2,1,0:T(8,128)(2,1)S(1)} %convert_element_type.163) | data formatting | bytes 983040 | tf_op jit(solution)/shard_map/convert_element_type | solution.py:70
  7.2 6.7 %reshape.281 = bf16[4,2,30720]{2,1,0:T(2,128)(2,1)} reshape(bf16[2560,2,3,16]{3,2,1,0:T(4,128)(2,1)} %bitcast.190) | data formatting | bytes 983040
  13.9 5.2 %all-to-all-start.1 = ((bf16[4,2,30720]{2,1,0:T(2,128)(2,1)}), bf16[4,2,30720]{2,1,0:T(2,128)(2,1)S(1)}, u32[]{:S(2)}, u32[]{:S(2)}) async-start(bf16[4,2,30720]{2,1,0:T(2,128)(2,1)} %reshape.281), calls=%async_computation.1 | async-start | bytes 983040 | tf_op jit(solution)/shard_map/all_to_all | solution.py:69
  19.1 5.2 %copy.82 = bf16[3,2,16,2560]{2,0,1,3:T(4,128)(2,1)} copy(bf16[3,2,16,2560]{3,2,1,0:T(8,128)(2,1)S(1)} %convert_element_type.162) | data formatting | bytes 983040 | tf_op jit(solution)/shard_map/convert_element_type | solution.py:67
  24.3 6.7 %reshape.279 = bf16[4,2,30720]{2,1,0:T(2,128)(2,1)} reshape(bf16[2560,2,3,16]{3,2,1,0:T(4,128)(2,1)} %bitcast.191) | data formatting | bytes 983040
  31.0 4.2 %all-to-all-start = ((bf16[4,2,30720]{2,1,0:T(2,128)(2,1)}), bf16[4,2,30720]{2,1,0:T(2,128)(2,1)S(1)}, u32[]{:S(2)}, u32[]{:S(2)}) async-start(bf16[4,2,30720]{2,1,0:T(2,128)(2,1)} %reshape.279), calls=%async_computation | async-start | bytes 983040 | tf_op jit(solution)/shard_map/all_to_all | solution.py:66
  35.8 6.0 %reshape.282 = bf16[2560,2,3,16]{3,2,1,0:T(4,128)(2,1)} reshape(bf16[4,2,30720]{2,1,0:T(2,128)(2,1)S(1)} %all-to-all-done.1) | data formatting | bytes 983040
  41.8 5.8 %copy.85 = bf16[3,2,16,4,640]{4,2,3,1,0:T(8,128)(2,1)S(1)} copy(bf16[3,2,16,4,640]{2,0,1,4,3:T(4,128)(2,1)} %bitcast.192) | data formatting | bytes 983040 | tf_op jit(solution)/shard_map/all_to_all | solution.py:69
  47.5 6.0 %reshape.280 = bf16[2560,2,3,16]{3,2,1,0:T(4,128)(2,1)} reshape(bf16[4,2,30720]{2,1,0:T(2,128)(2,1)S(1)} %all-to-all-done) | data formatting | bytes 983040
  53.5 5.8 %copy.83 = bf16[3,2,16,4,640]{4,2,3,1,0:T(8,128)(2,1)S(1)} copy(bf16[3,2,16,4,640]{2,0,1,4,3:T(4,128)(2,1)} %bitcast.193) | data formatting | bytes 983040 | tf_op jit(solution)/shard_map/all_to_all | solution.py:66
  63.5 4.2 %all-to-all-start.2 = ((bf16[3,2,64,640]{3,1,0,2:T(2,128)(2,1)}), bf16[3,2,64,640]{3,1,0,2:T(2,128)(2,1)S(1)}, u32[]{:S(2)}, u32[]{:S(2)}) async-start(bf16[3,2,64,640]{3,1,0,2:T(2,128)(2,1)} %copy.86), calls=%async_computation.2 | async-start | bytes 983040 | tf_op jit(solution)/shard_map/all_to_all | solution.py:77
  67.9 2.8 %gather_fusion.1 = bf16[128,16,128]{2,0,1:T(8,128)(2,1)S(1)} fusion(bf16[16,128,128]{2,1,0:T(8,128)(2,1)S(1)} %copy-done, s32[1024]{0:T(1024)S(1)} %pad_clamp_fusion), kind=kCustom, calls=%fused_computation.1 | custom fusion | bytes 1049088 | tf_op jit(solution)/shard_map/jit(_take)/gather | solution.py:96
  70.6 24.7 %gather_fusion = bf16[128,16,2560]{2,0,1:T(8,128)(2,1)} fusion(bf16[16,128,2560]{2,1,0:T(8,128)(2,1)} %param.11, s32[1024]{0:T(1024)S(1)} %pad_clamp_fusion.1), kind=kCustom, calls=%fused_computation | custom fusion | bytes 20972032 | tf_op jit(solution)/shard_map/jit(_take)/gather | solution.py:95
  97.6 9.0 %fusion.20 = bf16[2,16,2560]{2,0,1:T(2,128)(2,1)S(1)} fusion(bf16[16,20,128,128]{3,2,1,0:T(8,128)(2,1)} %param.10, bf16[2,16,20,128]{3,2,1,0:T(8,128)(2,1)S(1)} %convert_element_type.172), kind=kOutput, calls=%fused_computation.22 | convolution fusion | flops 21053440 | bytes 10813440 | tf_op jit(solution)/shard_map/mkij,cmkj->cmki/dot_general | solution.py:85
  106.7 2.9 %fusion.26 = f32[2,16,128]{2,0,1:T(2,128)S(1)} fusion(bf16[2,16,2560]{2,0,1:T(2,128)(2,1)S(1)} %fusion.20, bf16[128,16,2560]{2,0,1:T(8,128)(2,1)S(1)} %copy-done.2, pred[128]{0:T(512)(128)(4,1)S(1)} %get-tuple-element.25), kind=kOutput, calls=%fused_computation.24 | convolution fusion | flops 26214400 | bytes 10666112 | tf_op jit(solution)/shard_map/mij,cmj->cmi/dot_general | solution.py:97
  109.5 12.5 %all_gather.24 = f32[2,16,1024]{2,0,1:T(2,128)S(1)} all-gather(f32[2,16,128]{2,0,1:T(2,128)S(1)} %fusion.26), channel_id=1, replica_groups=mesh['mode'=4,'mesh'=8] {'mesh'}, dimensions={2}, use_global_device_ids=true | all-gather | bytes 147456 | tf_op jit(solution)/shard_map/all_gather | solution.py:40
  122.9 9.3 %all_gather.25 = f32[2,16,1024]{2,0,1:T(2,128)S(1)} all-gather(f32[2,16,128]{2,0,1:T(2,128)S(1)} %fusion.35), channel_id=1, replica_groups=mesh['mode'=4,'mesh'=8] {'mesh'}, dimensions={2}, use_global_device_ids=true | all-gather | bytes 147456 | tf_op jit(solution)/shard_map/all_gather | solution.py:40
  133.0 10.6 %all_gather.26 = f32[2,16,1024]{2,0,1:T(2,128)S(1)} all-gather(f32[2,16,128]{2,0,1:T(2,128)S(1)} %fusion.34), channel_id=1, replica_groups=mesh['mode'=4,'mesh'=8] {'mesh'}, dimensions={2}, use_global_device_ids=true | all-gather | bytes 147456 | tf_op jit(solution)/shard_map/all_gather | solution.py:40
  144.4 9.3 %all_gather.27 = f32[2,16,1024]{2,0,1:T(2,128)S(1)} all-gather(f32[2,16,128]{2,0,1:T(2,128)S(1)} %fusion.33), channel_id=1, replica_groups=mesh['mode'=4,'mesh'=8] {'mesh'}, dimensions={2}, use_global_device_ids=true | all-gather | bytes 147456 | tf_op jit(solution)/shard_map/all_gather | solution.py:40
  154.3 10.3 %all_gather.28 = bf16[2,16,1024]{2,0,1:T(2,128)(2,1)S(1)} all-gather(bf16[2,16,128]{2,0,1:T(2,128)(2,1)S(1)} %convert_bitcast_fusion.2), channel_id=1, replica_groups=mesh['mode'=4,'mesh'=8] {'mesh'}, dimensions={2}, use_global_device_ids=true | all-gather | bytes 73728 | tf_op jit(solution)/shard_map/all_gather | solution.py:44
  165.1 9.0 %all_gather.29 = bf16[2,16,1024]{2,0,1:T(2,128)(2,1)S(1)} all-gather(bf16[2,16,128]{2,0,1:T(2,128)(2,1)S(1)} %convert_bitcast_fusion.1), channel_id=1, replica_groups=mesh['mode'=4,'mesh'=8] {'mesh'}, dimensions={2}, use_global_device_ids=true | all-gather | bytes 73728 | tf_op jit(solution)/shard_map/all_gather | solution.py:44
  174.6 10.3 %all_gather.30 = bf16[2,16,1024]{2,0,1:T(2,128)(2,1)S(1)} all-gather(bf16[2,16,128]{2,0,1:T(2,128)(2,1)S(1)} %convert_bitcast_fusion), channel_id=1, replica_groups=mesh['mode'=4,'mesh'=8] {'mesh'}, dimensions={2}, use_global_device_ids=true | all-gather | bytes 73728 | tf_op jit(solution)/shard_map/all_gather | solution.py:44
  186.0 9.1 %all_gather.31 = bf16[2,16,1024]{2,0,1:T(2,128)(2,1)S(1)} all-gather(bf16[2,16,128]{2,0,1:T(2,128)(2,1)S(1)} %get-tuple-element.30), channel_id=1, replica_groups=mesh['mode'=4,'mesh'=8] {'mesh'}, dimensions={2}, use_global_device_ids=true | all-gather | bytes 73728 | tf_op jit(solution)/shard_map/all_gather | solution.py:44
  195.1 9.3 %convolution_bitcast_fusion.2 = f32[2,16,20,128]{3,0,2,1:T(2,128)S(1)} fusion(bf16[16,20,128,128]{3,2,1,0:T(8,128)(2,1)} %param.10, bf16[128,16,2560]{2,0,1:T(8,128)(2,1)} %gather_fusion, pred[128]{0:T(512)(128)(4,1)S(1)} %get-tuple-element.25, bf16[2,16,2560]{2,0,1:T(2,128)(2,1)S(1)} %fusion.20, bf16[2,16,1024]{2,0,1:T(2,128)(2,1)S(1)} %all_gather.31, ...), kind=kOutput, calls=%fused_computation.20 | convolution fusion | flops 47431680 | bytes 21471748 | tf_op jit(solution)/shard_map/mkji,cmkj->cmki/dot_general | solution.py:165
  (54 shorter events, 14.4 us)
Async XLA Ops:
  0.6 67.2 %copy-start = (bf16[16,128,128]{2,1,0:T(8,128)(2,1)S(1)}, bf16[16,128,128]{2,1,0:T(8,128)(2,1)}, u32[]{:S(2)}) copy-start(bf16[16,128,128]{2,1,0:T(8,128)(2,1)} %param.13) | copy-start | bytes 1572868
  0.6 18.4 %copy-start.4 = (f32[3,2,16,2560]{3,2,1,0:T(8,128)S(1)}, f32[3,2,16,2560]{3,2,1,0:T(8,128)}, u32[]{:S(2)}) copy-start(f32[3,2,16,2560]{3,2,1,0:T(8,128)} %param.8) | copy-start | bytes 2949124
  7.2 23.8 %copy-start.6 = (s32[1,2,128]{2,1,0:T(2,128)S(1)}, s32[1,2,128]{2,1,0:T(2,128)}, u32[]{:S(2)}) copy-start(s32[1,2,128]{2,1,0:T(2,128)} %param.15) | copy-start | bytes 3076
  13.9 17.1 %all-to-all-start.1 = ((bf16[4,2,30720]{2,1,0:T(2,128)(2,1)}), bf16[4,2,30720]{2,1,0:T(2,128)(2,1)S(1)}, u32[]{:S(2)}, u32[]{:S(2)}) async-start(bf16[4,2,30720]{2,1,0:T(2,128)(2,1)} %reshape.281), calls=%async_computation.1 | async-start | bytes 983040 | tf_op jit(solution)/shard_map/all_to_all | solution.py:69
  31.0 16.5 %all-to-all-start = ((bf16[4,2,30720]{2,1,0:T(2,128)(2,1)}), bf16[4,2,30720]{2,1,0:T(2,128)(2,1)S(1)}, u32[]{:S(2)}, u32[]{:S(2)}) async-start(bf16[4,2,30720]{2,1,0:T(2,128)(2,1)} %reshape.279), calls=%async_computation | async-start | bytes 983040 | tf_op jit(solution)/shard_map/all_to_all | solution.py:66
  63.5 31.8 %all-to-all-start.2 = ((bf16[3,2,64,640]{3,1,0,2:T(2,128)(2,1)}), bf16[3,2,64,640]{3,1,0,2:T(2,128)(2,1)S(1)}, u32[]{:S(2)}, u32[]{:S(2)}) async-start(bf16[3,2,64,640]{3,1,0,2:T(2,128)(2,1)} %copy.86), calls=%async_computation.2 | async-start | bytes 983040 | tf_op jit(solution)/shard_map/all_to_all | solution.py:77
  96.6 10.1 %copy-start.2 = (bf16[128,16,2560]{2,0,1:T(8,128)(2,1)S(1)}, bf16[128,16,2560]{2,0,1:T(8,128)(2,1)}, u32[]{:S(2)}) copy-start(bf16[128,16,2560]{2,0,1:T(8,128)(2,1)} %gather_fusion) | copy-start | bytes 31457284
  106.6 15.4 %copy-start.3 = (bf16[16,128,128]{2,1,0:T(8,128)(2,1)S(1)}, bf16[16,128,128]{2,1,0:T(8,128)(2,1)}, u32[]{:S(2)}) copy-start(bf16[16,128,128]{2,1,0:T(8,128)(2,1)} %param.12) | copy-start | bytes 1572868
  106.6 15.4 %copy-start.5 = (f32[2,16,128]{2,1,0:T(8,128)S(1)}, f32[2,16,128]{2,1,0:T(8,128)}, u32[]{:S(2)}) copy-start(f32[2,16,128]{2,1,0:T(8,128)} %param.14) | copy-start | bytes 49156
  186.0 19.3 %copy-start.1 = (bf16[16,128,128]{2,1,0:T(8,128)(2,1)S(1)}, bf16[16,128,128]{2,1,0:T(8,128)(2,1)}, u32[]{:S(2)}) copy-start(bf16[16,128,128]{2,1,0:T(8,128)(2,1)} %param.13) | copy-start | bytes 1572868
where the time goes:
time: 206 us; the launch traced here: 205 us
  blocking collectives  80.5 us (39%)
  local copies, waits for them, and re-layouts  78.6 us (38%)
  matrix products  28.4 us (14%)
  starting transfers between devices  13.6 us (7%)
  other arithmetic  3.23 us (2%)
    all_gather x4, blocking collectives, gather_children(): return lax.all_gather(values, 'mesh', axis=2, tiled=True)  41.7 us
    all_gather x4, blocking collectives, gather_parents(): return lax.all_gather(values, 'mesh', axis=2, tiled=True)  38.7 us
    unnamed x19, local copies, waits for them, and re-layouts  25.9 us
    gather x1, local copies, waits for them, and re-layouts, shards(): leaf_map = jnp.take(leaf_coupling, row_order[0], axis=1)  24.7 us
    dot_general x1, matrix products, shards(): jnp.einsum('mkji,cmkj->cmki', leaf_inverse, residue.astype(jnp.bfloat16)....  9.34 us
    dot_general x1, matrix products, shards(): jnp.einsum('mkij,cmkj->cmki', leaf_inverse, source.reshape(2, modes_dev,...  8.98 us
    all_to_all x1, local copies, waits for them, and re-layouts, shards(): lax.all_to_all(magnetic.astype(jnp.bfloat16), 'mode', split_axis=3, conca...  5.77 us
    all_to_all x1, local copies, waits for them, and re-layouts, shards(): lax.all_to_all(velocity.astype(jnp.bfloat16), 'mode', split_axis=3, conca...  5.77 us
  transfers between devices with their start and end apart: 3, of which 0 were waited for; matrix products, arithmetic and copies ran while one was open for 25% of the time, Pallas kernels for 0%

commit v1 on v0

--- a/solution.py
+++ b/solution.py
@@ -7,6 +7,29 @@
 NPHI = 192
 highest = lax.Precision.HIGHEST
 dt_step = 0.5
+
+
+def split_up(shard, dim, size):
+    shape = shard.shape
+    blocks = shard.reshape(*shape[:dim], size, shape[dim] // size, *shape[dim + 1 :])
+    return jnp.moveaxis(blocks, dim, 0)
+
+
+def joined_along(blocks, dim):
+    shape = list(blocks.shape[1:])
+    shape[dim] *= blocks.shape[0]
+    return jnp.moveaxis(blocks, 0, dim).reshape(shape)
+
+
+def rotated_exchange(shard, axis, split_dim, concat_dim):
+    count, index = (lax.axis_size(axis), lax.axis_index(axis))
+    blocks = split_up(shard, split_dim, count)
+    outs = [blocks[index]]
+    for lap in range(1, count):
+        sent = blocks[(index + lap) % count]
+        outs.append(lax.ppermute(sent, axis, [(i, (i + lap) % count) for i in range(count)]))
+    blocks = jnp.stack(outs)[(index - jnp.arange(count)) % count]
+    return joined_along(blocks, concat_dim)
 
 
 def tables():
@@ -66,9 +89,7 @@
         lax.all_to_all(
             velocity.astype(jnp.bfloat16), "mode", split_axis=3, concat_axis=2, tiled=True
         ).astype(velocity.dtype),
-        lax.all_to_all(
-            magnetic.astype(jnp.bfloat16), "mode", split_axis=3, concat_axis=2, tiled=True
-        ).astype(magnetic.dtype),
+        rotated_exchange(magnetic.astype(jnp.bfloat16), "mode", 3, 2).astype(magnetic.dtype),
     )
     phys_velocity, phys_magnetic = forward_fields(forward, spread_velocity, spread_magnetic)
     local_terms = jnp.einsum(

time: 206 us -> 190 us (0.922)
  local copies, waits for them, and re-layouts: 78.6 us -> 56.9 us
  waiting for transfers between devices: 0.01 us -> 4.8 us
    unnamed x19 -> x17, local copies, waits for them, and re-layouts: 25.9 us -> 13.3 us
    ppermute x0 -> x3, starting transfers between devices: none -> 6.09 us  [rotated_exchange(): lax.ppermute(sent, axis, [(i, (i + lap) % count) for i in range(count)])]
    all_to_all x1 -> x0, local copies, waits for them, and re-layouts: 5.77 us -> none  [shards(): lax.all_to_all(magnetic.astype(jnp.bfloat16), 'mode', split_axis=3, conca...]
    all_to_all x1 -> x0, starting transfers between devices: 5.19 us -> none  [shards(): lax.all_to_all(magnetic.astype(jnp.bfloat16), 'mode', split_axis=3, conca...]
    convert_element_type x1 -> x0, local copies, waits for them, and re-layouts: 5.18 us -> none  [shards(): magnetic.astype(jnp.bfloat16)]
    all_to_all x1, waiting for transfers between devices: 0.01 us -> 4.79 us  [shards(): lax.all_to_all(velocity.astype(jnp.bfloat16), 'mode', split_axis=3, conca...]
  transfers between devices with their start and end apart: 3 -> 5, of which waited for: 0 -> 1; matrix products, arithmetic and copies ran while one was open for 25% -> 23% of each run, Pallas kernels for 0% -> 0%
where the time goes in v1:
time: 190 us; the launch traced here: 189 us
  blocking collectives  80.3 us (42%)
  local copies, waits for them, and re-layouts  56.9 us (30%)
  matrix products  28.4 us (15%)
  starting transfers between devices  13 us (7%)
  waiting for transfers between devices  4.8 us (3%)
  other arithmetic  4.55 us (2%)
    all_gather x4, blocking collectives, gather_children(): return lax.all_gather(values, 'mesh', axis=2, tiled=True)  41.7 us
    all_gather x4, blocking collectives, gather_parents(): return lax.all_gather(values, 'mesh', axis=2, tiled=True)  38.6 us
    gather x1, local copies, waits for them, and re-layouts, shards(): leaf_map = jnp.take(leaf_coupling, row_order[0], axis=1)  24.7 us
    unnamed x17, local copies, waits for them, and re-layouts  13.3 us
    dot_general x1, matrix products, shards(): jnp.einsum('mkji,cmkj->cmki', leaf_inverse, residue.astype(jnp.bfloat16)....  9.34 us
    dot_general x1, matrix products, shards(): jnp.einsum('mkij,cmkj->cmki', leaf_inverse, source.reshape(2, modes_dev,...  8.98 us
    ppermute x3, starting transfers between devices, rotated_exchange(): lax.ppermute(sent, axis, [(i, (i + lap) % count) for i in range(count)])  6.09 us
    all_to_all x1, local copies, waits for them, and re-layouts, shards(): lax.all_to_all(velocity.astype(jnp.bfloat16), 'mode', split_axis=3, conca...  5.77 us
  transfers between devices with their start and end apart: 5, of which 1 were waited for; matrix products, arithmetic and copies ran while one was open for 23% of the time, Pallas kernels for 0%

profile of v1, /device:TPU:0, one launch (start us, length us, event | category | flops | bytes accessed | tf_op | source)
XLA Modules:
  0.0 189.1 jit_solution(10231111810536779350)
XLA Ops:
  0.7 1.3 convert_element_type.163
  3.2 3.0 %collective-permute-start = (bf16[3,2,16,640]{3,2,1,0:T(8,128)(2,1)S(1)}, bf16[3,2,16,640]{3,2,1,0:T(8,128)(2,1)S(1)}, u32[]{:S(2)}, u32[]{:S(2)}) collective-permute-start(bf16[3,2,16,640]{3,2,1,0:T(8,128)(2,1)S(1)} %bitcast.217), channel_id=1, source_target_pairs={{0,8},{8,16},{16,24},{24,0},{1,9},{9,17},{17,25},{25,1},{2,10},{10... | collective-permute-start | bytes 368648 | tf_op jit(solution)/shard_map/ppermute | solution.py:30
  6.2 1.6 collective-permute-start.1
  7.8 1.5 collective-permute-start.2
  10.6 5.2 %copy.90 = bf16[3,2,16,2560]{2,0,1,3:T(4,128)(2,1)} copy(bf16[3,2,16,2560]{3,2,1,0:T(8,128)(2,1)S(1)} %convert_element_type.162) | data formatting | bytes 983040 | tf_op jit(solution)/shard_map/convert_element_type | solution.py:90
  15.8 6.7 %reshape.351 = bf16[4,2,30720]{2,1,0:T(2,128)(2,1)} reshape(bf16[2560,2,3,16]{3,2,1,0:T(4,128)(2,1)} %bitcast.205) | data formatting | bytes 983040
  22.4 3.5 %all-to-all-start = ((bf16[4,2,30720]{2,1,0:T(2,128)(2,1)}), bf16[4,2,30720]{2,1,0:T(2,128)(2,1)S(1)}, u32[]{:S(2)}, u32[]{:S(2)}) async-start(bf16[4,2,30720]{2,1,0:T(2,128)(2,1)} %reshape.351), calls=%async_computation | async-start | bytes 983040 | tf_op jit(solution)/shard_map/all_to_all | solution.py:89
  28.2 4.8 %all-to-all-done = bf16[4,2,30720]{2,1,0:T(2,128)(2,1)S(1)} async-done(((bf16[4,2,30720]{2,1,0:T(2,128)(2,1)}), bf16[4,2,30720]{2,1,0:T(2,128)(2,1)S(1)}, u32[]{:S(2)}, u32[]{:S(2)}) %all-to-all-start) | async-done | bytes 491552 | tf_op jit(solution)/shard_map/all_to_all | solution.py:89
  33.0 6.0 %reshape.352 = bf16[2560,2,3,16]{3,2,1,0:T(4,128)(2,1)} reshape(bf16[4,2,30720]{2,1,0:T(2,128)(2,1)S(1)} %all-to-all-done) | data formatting | bytes 983040
  38.9 5.8 %copy.91 = bf16[3,2,16,4,640]{4,2,3,1,0:T(8,128)(2,1)S(1)} copy(bf16[3,2,16,4,640]{2,0,1,4,3:T(4,128)(2,1)} %bitcast.206) | data formatting | bytes 983040 | tf_op jit(solution)/shard_map/all_to_all | solution.py:89
  48.2 3.5 %all-to-all-start.1 = ((bf16[3,2,64,640]{3,1,0,2:T(2,128)(2,1)}), bf16[3,2,64,640]{3,1,0,2:T(2,128)(2,1)S(1)}, u32[]{:S(2)}, u32[]{:S(2)}) async-start(bf16[3,2,64,640]{3,1,0,2:T(2,128)(2,1)} %copy.93), calls=%async_computation.1 | async-start | bytes 983040 | tf_op jit(solution)/shard_map/all_to_all | solution.py:98
  51.8 2.8 %gather_fusion.2 = bf16[128,16,128]{2,0,1:T(8,128)(2,1)S(1)} fusion(bf16[16,128,128]{2,1,0:T(8,128)(2,1)S(1)} %copy-done, s32[1024]{0:T(1024)S(1)} %pad_clamp_fusion), kind=kCustom, calls=%fused_computation.2 | custom fusion | bytes 1049088 | tf_op jit(solution)/shard_map/jit(_take)/gather | solution.py:117
  54.6 24.7 %gather_fusion.1 = bf16[128,16,2560]{2,0,1:T(8,128)(2,1)} fusion(bf16[16,128,2560]{2,1,0:T(8,128)(2,1)} %param.11, s32[1024]{0:T(1024)S(1)} %pad_clamp_fusion.1), kind=kCustom, calls=%fused_computation.1 | custom fusion | bytes 20972032 | tf_op jit(solution)/shard_map/jit(_take)/gather | solution.py:116
  81.6 9.0 %fusion.20 = bf16[2,16,2560]{2,0,1:T(2,128)(2,1)S(1)} fusion(bf16[16,20,128,128]{3,2,1,0:T(8,128)(2,1)} %param.10, bf16[2,16,20,128]{3,2,1,0:T(8,128)(2,1)S(1)} %convert_element_type.172), kind=kOutput, calls=%fused_computation.23 | convolution fusion | flops 21053440 | bytes 10813440 | tf_op jit(solution)/shard_map/mkij,cmkj->cmki/dot_general | solution.py:106
  90.6 2.9 %fusion.26 = f32[2,16,128]{2,0,1:T(2,128)S(1)} fusion(bf16[2,16,2560]{2,0,1:T(2,128)(2,1)S(1)} %fusion.20, bf16[128,16,2560]{2,0,1:T(8,128)(2,1)S(1)} %copy-done.1, pred[128]{0:T(512)(128)(4,1)S(1)} %get-tuple-element.32), kind=kOutput, calls=%fused_computation.25 | convolution fusion | flops 26214400 | bytes 10666112 | tf_op jit(solution)/shard_map/mij,cmj->cmi/dot_general | solution.py:118
  93.5 12.5 %all_gather.24 = f32[2,16,1024]{2,0,1:T(2,128)S(1)} all-gather(f32[2,16,128]{2,0,1:T(2,128)S(1)} %fusion.26), channel_id=1, replica_groups=mesh['mode'=4,'mesh'=8] {'mesh'}, dimensions={2}, use_global_device_ids=true | all-gather | bytes 147456 | tf_op jit(solution)/shard_map/all_gather | solution.py:63
  106.8 9.3 %all_gather.25 = f32[2,16,1024]{2,0,1:T(2,128)S(1)} all-gather(f32[2,16,128]{2,0,1:T(2,128)S(1)} %fusion.35), channel_id=1, replica_groups=mesh['mode'=4,'mesh'=8] {'mesh'}, dimensions={2}, use_global_device_ids=true | all-gather | bytes 147456 | tf_op jit(solution)/shard_map/all_gather | solution.py:63
  116.9 10.6 %all_gather.26 = f32[2,16,1024]{2,0,1:T(2,128)S(1)} all-gather(f32[2,16,128]{2,0,1:T(2,128)S(1)} %fusion.34), channel_id=1, replica_groups=mesh['mode'=4,'mesh'=8] {'mesh'}, dimensions={2}, use_global_device_ids=true | all-gather | bytes 147456 | tf_op jit(solution)/shard_map/all_gather | solution.py:63
  128.4 9.3 %all_gather.27 = f32[2,16,1024]{2,0,1:T(2,128)S(1)} all-gather(f32[2,16,128]{2,0,1:T(2,128)S(1)} %fusion.33), channel_id=1, replica_groups=mesh['mode'=4,'mesh'=8] {'mesh'}, dimensions={2}, use_global_device_ids=true | all-gather | bytes 147456 | tf_op jit(solution)/shard_map/all_gather | solution.py:63
  138.3 10.3 %all_gather.28 = bf16[2,16,1024]{2,0,1:T(2,128)(2,1)S(1)} all-gather(bf16[2,16,128]{2,0,1:T(2,128)(2,1)S(1)} %convert_bitcast_fusion.2), channel_id=1, replica_groups=mesh['mode'=4,'mesh'=8] {'mesh'}, dimensions={2}, use_global_device_ids=true | all-gather | bytes 73728 | tf_op jit(solution)/shard_map/all_gather | solution.py:67
  149.1 9.0 %all_gather.29 = bf16[2,16,1024]{2,0,1:T(2,128)(2,1)S(1)} all-gather(bf16[2,16,128]{2,0,1:T(2,128)(2,1)S(1)} %convert_bitcast_fusion.1), channel_id=1, replica_groups=mesh['mode'=4,'mesh'=8] {'mesh'}, dimensions={2}, use_global_device_ids=true | all-gather | bytes 73728 | tf_op jit(solution)/shard_map/all_gather | solution.py:67
  158.5 10.3 %all_gather.30 = bf16[2,16,1024]{2,0,1:T(2,128)(2,1)S(1)} all-gather(bf16[2,16,128]{2,0,1:T(2,128)(2,1)S(1)} %convert_bitcast_fusion), channel_id=1, replica_groups=mesh['mode'=4,'mesh'=8] {'mesh'}, dimensions={2}, use_global_device_ids=true | all-gather | bytes 73728 | tf_op jit(solution)/shard_map/all_gather | solution.py:67
  169.9 9.0 %all_gather.31 = bf16[2,16,1024]{2,0,1:T(2,128)(2,1)S(1)} all-gather(bf16[2,16,128]{2,0,1:T(2,128)(2,1)S(1)} %get-tuple-element.37), channel_id=1, replica_groups=mesh['mode'=4,'mesh'=8] {'mesh'}, dimensions={2}, use_global_device_ids=true | all-gather | bytes 73728 | tf_op jit(solution)/shard_map/all_gather | solution.py:67
  178.9 9.3 %convolution_bitcast_fusion.2 = f32[2,16,20,128]{3,0,2,1:T(2,128)S(1)} fusion(bf16[16,20,128,128]{3,2,1,0:T(8,128)(2,1)} %param.10, bf16[128,16,2560]{2,0,1:T(8,128)(2,1)} %gather_fusion.1, pred[128]{0:T(512)(128)(4,1)S(1)} %get-tuple-element.32, bf16[2,16,2560]{2,0,1:T(2,128)(2,1)S(1)} %fusion.20, bf16[2,16,1024]{2,0,1:T(2,128)(2,1)S(1)} %all_gather.31, ...), kind=kOutput, calls=%fused_computation.21 | convolution fusion | flops 47431680 | bytes 21471748 | tf_op jit(solution)/shard_map/mkji,cmkj->cmki/dot_general | solution.py:186
  (61 shorter events, 16.3 us)
Async XLA Ops:
  0.6 51.2 %copy-start = (bf16[16,128,128]{2,1,0:T(8,128)(2,1)S(1)}, bf16[16,128,128]{2,1,0:T(8,128)(2,1)}, u32[]{:S(2)}) copy-start(bf16[16,128,128]{2,1,0:T(8,128)(2,1)} %param.13) | copy-start | bytes 1572868
  0.6 25.5 %copy-start.4 = (s32[1,2,128]{2,1,0:T(2,128)S(1)}, s32[1,2,128]{2,1,0:T(2,128)}, u32[]{:S(2)}) copy-start(s32[1,2,128]{2,1,0:T(2,128)} %param.15) | copy-start | bytes 3076
  3.2 23.4 %collective-permute-start = (bf16[3,2,16,640]{3,2,1,0:T(8,128)(2,1)S(1)}, bf16[3,2,16,640]{3,2,1,0:T(8,128)(2,1)S(1)}, u32[]{:S(2)}, u32[]{:S(2)}) collective-permute-start(bf16[3,2,16,640]{3,2,1,0:T(8,128)(2,1)S(1)} %bitcast.217), channel_id=1, source_target_pairs={{0,8},{8,16},{16,24},{24,0},{1,9},{9,17},{17,25},{25,1},{2,10},{10... | collective-permute-start | bytes 368648 | tf_op jit(solution)/shard_map/ppermute | solution.py:30
  6.2 20.3 %collective-permute-start.1 = (bf16[3,2,16,640]{3,2,1,0:T(8,128)(2,1)S(1)}, bf16[3,2,16,640]{3,2,1,0:T(8,128)(2,1)S(1)}, u32[]{:S(2)}, u32[]{:S(2)}) collective-permute-start(bf16[3,2,16,640]{3,2,1,0:T(8,128)(2,1)S(1)} %bitcast.218), channel_id=1, source_target_pairs={{0,16},{8,24},{16,0},{24,8},{1,17},{9,25},{17,1},{25,9},{2,18},{10... | collective-permute-start | bytes 368648 | tf_op jit(solution)/shard_map/ppermute | solution.py:30
  7.8 18.7 %collective-permute-start.2 = (bf16[3,2,16,640]{3,2,1,0:T(8,128)(2,1)S(1)}, bf16[3,2,16,640]{3,2,1,0:T(8,128)(2,1)S(1)}, u32[]{:S(2)}, u32[]{:S(2)}) collective-permute-start(bf16[3,2,16,640]{3,2,1,0:T(8,128)(2,1)S(1)} %bitcast.220), channel_id=1, source_target_pairs={{0,24},{8,0},{16,8},{24,16},{1,25},{9,1},{17,9},{25,17},{2,26},{10... | collective-permute-start | bytes 368648 | tf_op jit(solution)/shard_map/ppermute | solution.py:30
  22.4 10.5 %all-to-all-start = ((bf16[4,2,30720]{2,1,0:T(2,128)(2,1)}), bf16[4,2,30720]{2,1,0:T(2,128)(2,1)S(1)}, u32[]{:S(2)}, u32[]{:S(2)}) async-start(bf16[4,2,30720]{2,1,0:T(2,128)(2,1)} %reshape.351), calls=%async_computation | async-start | bytes 983040 | tf_op jit(solution)/shard_map/all_to_all | solution.py:89
  48.2 31.1 %all-to-all-start.1 = ((bf16[3,2,64,640]{3,1,0,2:T(2,128)(2,1)}), bf16[3,2,64,640]{3,1,0,2:T(2,128)(2,1)S(1)}, u32[]{:S(2)}, u32[]{:S(2)}) async-start(bf16[3,2,64,640]{3,1,0,2:T(2,128)(2,1)} %copy.93), calls=%async_computation.1 | async-start | bytes 983040 | tf_op jit(solution)/shard_map/all_to_all | solution.py:98
  80.5 10.1 %copy-start.1 = (bf16[128,16,2560]{2,0,1:T(8,128)(2,1)S(1)}, bf16[128,16,2560]{2,0,1:T(8,128)(2,1)}, u32[]{:S(2)}) copy-start(bf16[128,16,2560]{2,0,1:T(8,128)(2,1)} %gather_fusion.1) | copy-start | bytes 31457284
  90.6 15.4 %copy-start.2 = (bf16[16,128,128]{2,1,0:T(8,128)(2,1)S(1)}, bf16[16,128,128]{2,1,0:T(8,128)(2,1)}, u32[]{:S(2)}) copy-start(bf16[16,128,128]{2,1,0:T(8,128)(2,1)} %param.12) | copy-start | bytes 1572868
  90.6 15.4 %copy-start.3 = (f32[2,16,128]{2,1,0:T(8,128)S(1)}, f32[2,16,128]{2,1,0:T(8,128)}, u32[]{:S(2)}) copy-start(f32[2,16,128]{2,1,0:T(8,128)} %param.14) | copy-start | bytes 49156
